TPU v7x, 32 devices: a whole 2x2x4 slice. The times are simulated.
32 devices in a mesh: prow: 4 (over y, core), pcol: 8 (over z, x).
Axes of the slice: x: 2, y: 2, z: 4, core: 2. Of those that a mesh axis runs over, the one named last changes fastest.
Arguments:
- inverse_cov: bfloat16 [8192, 8192], P('prow', 'pcol'), may hold values from -0.5 to 4.5, as said below
- cosines: float32 [8192, 8192], P('prow', 'pcol'), may hold values from -1 to 1, as said below
- sky_maps: bfloat16 [8192, 192], P('pcol'), may hold values from -6 to 6
Outputs:
- filtered: bfloat16 [8192, 192], P('prow')
- spectra: float32 [64, 192], replicated
Inputs may be any that keep to these rules, and one draw needn't show every extreme that they name: `inverse_cov`: symmetric, with a dominant diagonal. `cosines`: symmetric.
All inputs are finite; a program needn't handle non-finite values.
Results may differ from a plain program's by a relative error of at most 0.0033.
Values may be sent and summed in bfloat16 or wider, within the bound.
A program may use at most 128 MiB of HBM per device.

v0:
```python
import jax
import jax.numpy as jnp
from jax import lax
from jax.sharding import PartitionSpec as P

NPIX = 8192
L = 64
LMIN = 2
GROUP = 4


def next_legendre(previous, current, cosine, degree):
    return ((2.0 * degree - 1.0) * cosine * current - (degree - 1.0) * previous) / degree


def per_device(inverse_cov, cosines, sky_maps):
    cols_here = inverse_cov.shape[1]
    partial_value = jnp.dot(inverse_cov, sky_maps, preferred_element_type=jnp.float32)
    filtered = lax.psum(partial_value, "pcol").astype(jnp.bfloat16)
    column_index = lax.axis_index("pcol")
    full_maps = lax.all_gather(filtered, "prow", axis=0, tiled=True)
    filtered_cols = lax.dynamic_slice_in_dim(full_maps, column_index * cols_here, cols_here, 0)
    rows_f32 = filtered.astype(jnp.float32)
    previous = jnp.ones_like(cosines)
    current = cosines

    def advance(carried, turn_index):
        previous, current = carried
        term_list = []
        weights = []
        for offset in range(GROUP):
            degree = (LMIN + turn_index * GROUP + offset).astype(jnp.float32)
            next_term = next_legendre(previous, current, cosines, degree)
            term_list.append(next_term.astype(jnp.bfloat16))
            weights.append((2.0 * degree + 1.0) / NPIX)
            previous, current = (current, next_term)
        stacked = jnp.stack(term_list)
        product = jnp.einsum(
            "grc,cm->grm", stacked, filtered_cols, preferred_element_type=jnp.float32
        )
        quadratic = jnp.sum(product * rows_f32[None], axis=1)
        return ((previous, current), quadratic * jnp.stack(weights)[:, None])

    carried, partial_spectra = lax.scan(
        advance, (previous, current), jnp.arange(L // GROUP, dtype=jnp.int32)
    )
    spectra = lax.psum(partial_spectra.reshape(L, -1), ("prow", "pcol"))
    return (filtered, spectra)


def solution(mesh):
    in_specs = (P("prow", "pcol"), P("prow", "pcol"), P("pcol", None))
    out_specs = (P("prow", None), P())
    return jax.shard_map(
        per_device, mesh=mesh, in_specs=in_specs, out_specs=out_specs, check_vma=False
    )
```

profile of v0, /device:TPU:0, one launch (start us, length us, event | category | flops | bytes accessed | tf_op | source)
XLA Modules:
  0.0 855.3 jit_solution(4507010402875812031)
XLA Ops:
  11.9 82.8 %all-reduce.1 = bf16[2048,192]{0,1:T(8,128)(2,1)} all-reduce(f32[2048,192]{0,1:T(8,128)S(1)} %fusion.15), channel_id=1, replica_groups=mesh['prow'=4,'pcol'=8] {'pcol'}, use_global_device_ids=true, to_apply=%region_0.0 | all-reduce | flops 393216 | bytes 2359296 | tf_op jit(solution)/shard_map/psum | solution.py:19
  105.7 16.7 %all-gather.2.cloned.1.call-done = bf16[8192,192]{0,1:T(8,128)(2,1)} async-done(((bf16[2048,192]{0,1:T(8,128)(2,1)}), bf16[8192,192]{0,1:T(8,128)(2,1)}) %all-gather.2.cloned.1.call-update) | async-done | bytes 3145744 | tf_op jit(solution)/shard_map/all_gather | solution.py:21
  123.5 684.9 %while.18 = (s32[]{:T(128)}, f32[2048,1024]{1,0:T(8,128)}, f32[2048,1024]{1,0:T(8,128)}, f32[16,4,192]{2,1,0:T(4,128)S(1)}, s32[16]{0:T(128)S(1)}, /*index=5*/f3...) while((s32[]{:T(128)}, f32[2048,1024]{1,0:T(8,128)}, ...), condition=%wide.region_3.4_spmd.clone, body=%wide.region_1.3_spmd.clone.sunk | while | flops 3325034496 | bytes 194916608 | solution.py:44
  162.9 12.4 %convert_bitcast_fusion.6 = (bf16[1,2048,1024]{2,1,0:T(8,128)(2,1)S(1)}, f32[2048,1024]{1,0:T(8,128)S(1)}, bf16[1,2048,1024]{2,1,0:T(8,128)(2,1)}) fusion(f32[]{:T(128)} %bitcast.41, f32[]{:T(128)S(6)} %sub.98, f32[]{:T(128)} %bitcast.42, f32[2048,1024]{1,0:T(8,128)} %get-tuple-element.271, f32[]{:T(128)S(6)} %sub.99, f32[]{:T(128)} %bitcast.43, ...), kind=kLoop, calls=%fused_computation.16.clone.1 | loop fusion | flops 37748736 | bytes 41943076 | tf_op jit(solution)/shard_map/while/body/eval_jaxpr/stack | solution.py:37
  175.3 14.8 %convert_bitcast_fusion.7 = (bf16[1,2048,1024]{2,1,0:T(8,128)(2,1)}, f32[2048,1024]{1,0:T(8,128)}, bf16[1,2048,1024]{2,1,0:T(8,128)(2,1)}) fusion(f32[]{:T(128)} %bitcast.44, f32[]{:T(128)} %bitcast.42, f32[2048,1024]{1,0:T(8,128)} %get-tuple-element.271, f32[]{:T(128)S(6)} %sub.99, f32[]{:T(128)} %bitcast.43, f32[2048,1024]{1,0:T(8,128)} %get-tuple-element.270, ...), kind=kLoop, calls=%fused_computation.15.clone.1 | loop fusion | flops 37748736 | bytes 50331684 | tf_op jit(solution)/shard_map/while/body/eval_jaxpr/stack | solution.py:37
  206.0 12.4 %convert_bitcast_fusion.6 = (bf16[1,2048,1024]{2,1,0:T(8,128)(2,1)S(1)}, f32[2048,1024]{1,0:T(8,128)S(1)}, bf16[1,2048,1024]{2,1,0:T(8,128)(2,1)}) fusion(f32[]{:T(128)} %bitcast.41, f32[]{:T(128)S(6)} %sub.98, f32[]{:T(128)} %bitcast.42, f32[2048,1024]{1,0:T(8,128)} %get-tuple-element.271, f32[]{:T(128)S(6)} %sub.99, f32[]{:T(128)} %bitcast.43, ...), kind=kLoop, calls=%fused_computation.16.clone.1 | loop fusion | flops 37748736 | bytes 41943076 | tf_op jit(solution)/shard_map/while/body/eval_jaxpr/stack | solution.py:37
  218.4 14.8 %convert_bitcast_fusion.7 = (bf16[1,2048,1024]{2,1,0:T(8,128)(2,1)}, f32[2048,1024]{1,0:T(8,128)}, bf16[1,2048,1024]{2,1,0:T(8,128)(2,1)}) fusion(f32[]{:T(128)} %bitcast.44, f32[]{:T(128)} %bitcast.42, f32[2048,1024]{1,0:T(8,128)} %get-tuple-element.271, f32[]{:T(128)S(6)} %sub.99, f32[]{:T(128)} %bitcast.43, f32[2048,1024]{1,0:T(8,128)} %get-tuple-element.270, ...), kind=kLoop, calls=%fused_computation.15.clone.1 | loop fusion | flops 37748736 | bytes 50331684 | tf_op jit(solution)/shard_map/while/body/eval_jaxpr/stack | solution.py:37
  249.1 12.4 %convert_bitcast_fusion.6 = (bf16[1,2048,1024]{2,1,0:T(8,128)(2,1)S(1)}, f32[2048,1024]{1,0:T(8,128)S(1)}, bf16[1,2048,1024]{2,1,0:T(8,128)(2,1)}) fusion(f32[]{:T(128)} %bitcast.41, f32[]{:T(128)S(6)} %sub.98, f32[]{:T(128)} %bitcast.42, f32[2048,1024]{1,0:T(8,128)} %get-tuple-element.271, f32[]{:T(128)S(6)} %sub.99, f32[]{:T(128)} %bitcast.43, ...), kind=kLoop, calls=%fused_computation.16.clone.1 | loop fusion | flops 37748736 | bytes 41943076 | tf_op jit(solution)/shard_map/while/body/eval_jaxpr/stack | solution.py:37
  261.5 14.8 %convert_bitcast_fusion.7 = (bf16[1,2048,1024]{2,1,0:T(8,128)(2,1)}, f32[2048,1024]{1,0:T(8,128)}, bf16[1,2048,1024]{2,1,0:T(8,128)(2,1)}) fusion(f32[]{:T(128)} %bitcast.44, f32[]{:T(128)} %bitcast.42, f32[2048,1024]{1,0:T(8,128)} %get-tuple-element.271, f32[]{:T(128)S(6)} %sub.99, f32[]{:T(128)} %bitcast.43, f32[2048,1024]{1,0:T(8,128)} %get-tuple-element.270, ...), kind=kLoop, calls=%fused_computation.15.clone.1 | loop fusion | flops 37748736 | bytes 50331684 | tf_op jit(solution)/shard_map/while/body/eval_jaxpr/stack | solution.py:37
  292.2 12.4 %convert_bitcast_fusion.6 = (bf16[1,2048,1024]{2,1,0:T(8,128)(2,1)S(1)}, f32[2048,1024]{1,0:T(8,128)S(1)}, bf16[1,2048,1024]{2,1,0:T(8,128)(2,1)}) fusion(f32[]{:T(128)} %bitcast.41, f32[]{:T(128)S(6)} %sub.98, f32[]{:T(128)} %bitcast.42, f32[2048,1024]{1,0:T(8,128)} %get-tuple-element.271, f32[]{:T(128)S(6)} %sub.99, f32[]{:T(128)} %bitcast.43, ...), kind=kLoop, calls=%fused_computation.16.clone.1 | loop fusion | flops 37748736 | bytes 41943076 | tf_op jit(solution)/shard_map/while/body/eval_jaxpr/stack | solution.py:37
  304.6 14.8 %convert_bitcast_fusion.7 = (bf16[1,2048,1024]{2,1,0:T(8,128)(2,1)}, f32[2048,1024]{1,0:T(8,128)}, bf16[1,2048,1024]{2,1,0:T(8,128)(2,1)}) fusion(f32[]{:T(128)} %bitcast.44, f32[]{:T(128)} %bitcast.42, f32[2048,1024]{1,0:T(8,128)} %get-tuple-element.271, f32[]{:T(128)S(6)} %sub.99, f32[]{:T(128)} %bitcast.43, f32[2048,1024]{1,0:T(8,128)} %get-tuple-element.270, ...), kind=kLoop, calls=%fused_computation.15.clone.1 | loop fusion | flops 37748736 | bytes 50331684 | tf_op jit(solution)/shard_map/while/body/eval_jaxpr/stack | solution.py:37
  335.3 12.4 %convert_bitcast_fusion.6 = (bf16[1,2048,1024]{2,1,0:T(8,128)(2,1)S(1)}, f32[2048,1024]{1,0:T(8,128)S(1)}, bf16[1,2048,1024]{2,1,0:T(8,128)(2,1)}) fusion(f32[]{:T(128)} %bitcast.41, f32[]{:T(128)S(6)} %sub.98, f32[]{:T(128)} %bitcast.42, f32[2048,1024]{1,0:T(8,128)} %get-tuple-element.271, f32[]{:T(128)S(6)} %sub.99, f32[]{:T(128)} %bitcast.43, ...), kind=kLoop, calls=%fused_computation.16.clone.1 | loop fusion | flops 37748736 | bytes 41943076 | tf_op jit(solution)/shard_map/while/body/eval_jaxpr/stack | solution.py:37
  347.8 14.8 %convert_bitcast_fusion.7 = (bf16[1,2048,1024]{2,1,0:T(8,128)(2,1)}, f32[2048,1024]{1,0:T(8,128)}, bf16[1,2048,1024]{2,1,0:T(8,128)(2,1)}) fusion(f32[]{:T(128)} %bitcast.44, f32[]{:T(128)} %bitcast.42, f32[2048,1024]{1,0:T(8,128)} %get-tuple-element.271, f32[]{:T(128)S(6)} %sub.99, f32[]{:T(128)} %bitcast.43, f32[2048,1024]{1,0:T(8,128)} %get-tuple-element.270, ...), kind=kLoop, calls=%fused_computation.15.clone.1 | loop fusion | flops 37748736 | bytes 50331684 | tf_op jit(solution)/shard_map/while/body/eval_jaxpr/stack | solution.py:37
  390.9 14.8 %convert_bitcast_fusion.7 = (bf16[1,2048,1024]{2,1,0:T(8,128)(2,1)}, f32[2048,1024]{1,0:T(8,128)}, bf16[1,2048,1024]{2,1,0:T(8,128)(2,1)}) fusion(f32[]{:T(128)} %bitcast.44, f32[]{:T(128)} %bitcast.42, f32[2048,1024]{1,0:T(8,128)} %get-tuple-element.271, f32[]{:T(128)S(6)} %sub.99, f32[]{:T(128)} %bitcast.43, f32[2048,1024]{1,0:T(8,128)} %get-tuple-element.270, ...), kind=kLoop, calls=%fused_computation.15.clone.1 | loop fusion | flops 37748736 | bytes 50331684 | tf_op jit(solution)/shard_map/while/body/eval_jaxpr/stack | solution.py:37
  434.0 14.8 %convert_bitcast_fusion.7 = (bf16[1,2048,1024]{2,1,0:T(8,128)(2,1)}, f32[2048,1024]{1,0:T(8,128)}, bf16[1,2048,1024]{2,1,0:T(8,128)(2,1)}) fusion(f32[]{:T(128)} %bitcast.44, f32[]{:T(128)} %bitcast.42, f32[2048,1024]{1,0:T(8,128)} %get-tuple-element.271, f32[]{:T(128)S(6)} %sub.99, f32[]{:T(128)} %bitcast.43, f32[2048,1024]{1,0:T(8,128)} %get-tuple-element.270, ...), kind=kLoop, calls=%fused_computation.15.clone.1 | loop fusion | flops 37748736 | bytes 50331684 | tf_op jit(solution)/shard_map/while/body/eval_jaxpr/stack | solution.py:37
  477.1 14.8 %convert_bitcast_fusion.7 = (bf16[1,2048,1024]{2,1,0:T(8,128)(2,1)}, f32[2048,1024]{1,0:T(8,128)}, bf16[1,2048,1024]{2,1,0:T(8,128)(2,1)}) fusion(f32[]{:T(128)} %bitcast.44, f32[]{:T(128)} %bitcast.42, f32[2048,1024]{1,0:T(8,128)} %get-tuple-element.271, f32[]{:T(128)S(6)} %sub.99, f32[]{:T(128)} %bitcast.43, f32[2048,1024]{1,0:T(8,128)} %get-tuple-element.270, ...), kind=kLoop, calls=%fused_computation.15.clone.1 | loop fusion | flops 37748736 | bytes 50331684 | tf_op jit(solution)/shard_map/while/body/eval_jaxpr/stack | solution.py:37
  520.2 14.8 %convert_bitcast_fusion.7 = (bf16[1,2048,1024]{2,1,0:T(8,128)(2,1)}, f32[2048,1024]{1,0:T(8,128)}, bf16[1,2048,1024]{2,1,0:T(8,128)(2,1)}) fusion(f32[]{:T(128)} %bitcast.44, f32[]{:T(128)} %bitcast.42, f32[2048,1024]{1,0:T(8,128)} %get-tuple-element.271, f32[]{:T(128)S(6)} %sub.99, f32[]{:T(128)} %bitcast.43, f32[2048,1024]{1,0:T(8,128)} %get-tuple-element.270, ...), kind=kLoop, calls=%fused_computation.15.clone.1 | loop fusion | flops 37748736 | bytes 50331684 | tf_op jit(solution)/shard_map/while/body/eval_jaxpr/stack | solution.py:37
  563.4 14.8 %convert_bitcast_fusion.7 = (bf16[1,2048,1024]{2,1,0:T(8,128)(2,1)}, f32[2048,1024]{1,0:T(8,128)}, bf16[1,2048,1024]{2,1,0:T(8,128)(2,1)}) fusion(f32[]{:T(128)} %bitcast.44, f32[]{:T(128)} %bitcast.42, f32[2048,1024]{1,0:T(8,128)} %get-tuple-element.271, f32[]{:T(128)S(6)} %sub.99, f32[]{:T(128)} %bitcast.43, f32[2048,1024]{1,0:T(8,128)} %get-tuple-element.270, ...), kind=kLoop, calls=%fused_computation.15.clone.1 | loop fusion | flops 37748736 | bytes 50331684 | tf_op jit(solution)/shard_map/while/body/eval_jaxpr/stack | solution.py:37
  606.5 14.8 %convert_bitcast_fusion.7 = (bf16[1,2048,1024]{2,1,0:T(8,128)(2,1)}, f32[2048,1024]{1,0:T(8,128)}, bf16[1,2048,1024]{2,1,0:T(8,128)(2,1)}) fusion(f32[]{:T(128)} %bitcast.44, f32[]{:T(128)} %bitcast.42, f32[2048,1024]{1,0:T(8,128)} %get-tuple-element.271, f32[]{:T(128)S(6)} %sub.99, f32[]{:T(128)} %bitcast.43, f32[2048,1024]{1,0:T(8,128)} %get-tuple-element.270, ...), kind=kLoop, calls=%fused_computation.15.clone.1 | loop fusion | flops 37748736 | bytes 50331684 | tf_op jit(solution)/shard_map/while/body/eval_jaxpr/stack | solution.py:37
  649.6 14.8 %convert_bitcast_fusion.7 = (bf16[1,2048,1024]{2,1,0:T(8,128)(2,1)}, f32[2048,1024]{1,0:T(8,128)}, bf16[1,2048,1024]{2,1,0:T(8,128)(2,1)}) fusion(f32[]{:T(128)} %bitcast.44, f32[]{:T(128)} %bitcast.42, f32[2048,1024]{1,0:T(8,128)} %get-tuple-element.271, f32[]{:T(128)S(6)} %sub.99, f32[]{:T(128)} %bitcast.43, f32[2048,1024]{1,0:T(8,128)} %get-tuple-element.270, ...), kind=kLoop, calls=%fused_computation.15.clone.1 | loop fusion | flops 37748736 | bytes 50331684 | tf_op jit(solution)/shard_map/while/body/eval_jaxpr/stack | solution.py:37
  692.7 14.8 %convert_bitcast_fusion.7 = (bf16[1,2048,1024]{2,1,0:T(8,128)(2,1)}, f32[2048,1024]{1,0:T(8,128)}, bf16[1,2048,1024]{2,1,0:T(8,128)(2,1)}) fusion(f32[]{:T(128)} %bitcast.44, f32[]{:T(128)} %bitcast.42, f32[2048,1024]{1,0:T(8,128)} %get-tuple-element.271, f32[]{:T(128)S(6)} %sub.99, f32[]{:T(128)} %bitcast.43, f32[2048,1024]{1,0:T(8,128)} %get-tuple-element.270, ...), kind=kLoop, calls=%fused_computation.15.clone.1 | loop fusion | flops 37748736 | bytes 50331684 | tf_op jit(solution)/shard_map/while/body/eval_jaxpr/stack | solution.py:37
  735.8 14.8 %convert_bitcast_fusion.7 = (bf16[1,2048,1024]{2,1,0:T(8,128)(2,1)}, f32[2048,1024]{1,0:T(8,128)}, bf16[1,2048,1024]{2,1,0:T(8,128)(2,1)}) fusion(f32[]{:T(128)} %bitcast.44, f32[]{:T(128)} %bitcast.42, f32[2048,1024]{1,0:T(8,128)} %get-tuple-element.271, f32[]{:T(128)S(6)} %sub.99, f32[]{:T(128)} %bitcast.43, f32[2048,1024]{1,0:T(8,128)} %get-tuple-element.270, ...), kind=kLoop, calls=%fused_computation.15.clone.1 | loop fusion | flops 37748736 | bytes 50331684 | tf_op jit(solution)/shard_map/while/body/eval_jaxpr/stack | solution.py:37
  779.0 14.8 %convert_bitcast_fusion.7 = (bf16[1,2048,1024]{2,1,0:T(8,128)(2,1)}, f32[2048,1024]{1,0:T(8,128)}, bf16[1,2048,1024]{2,1,0:T(8,128)(2,1)}) fusion(f32[]{:T(128)} %bitcast.44, f32[]{:T(128)} %bitcast.42, f32[2048,1024]{1,0:T(8,128)} %get-tuple-element.271, f32[]{:T(128)S(6)} %sub.99, f32[]{:T(128)} %bitcast.43, f32[2048,1024]{1,0:T(8,128)} %get-tuple-element.270, ...), kind=kLoop, calls=%fused_computation.15.clone.1 | loop fusion | flops 37748736 | bytes 50331684 | tf_op jit(solution)/shard_map/while/body/eval_jaxpr/stack | solution.py:37
  808.4 40.1 %psum.15 = f32[64,192]{1,0:T(8,128)} all-reduce(f32[64,192]{1,0:T(8,128)S(1)} %reshape.51), channel_id=1, replica_groups=mesh['prow'=4,'pcol'=8] {'prow','pcol'}, use_global_device_ids=true, to_apply=%region_4.5 | all-reduce | flops 12288 | bytes 98304 | tf_op jit(solution)/shard_map/psum | solution.py:47
  (200 shorter events, 406.7 us)
Async XLA Ops:
  7.2 115.2 %all-gather.2.cloned.1.call-start = ((), (), s32[]{:S(2)}) async-start(), calls=%async_computation | async-start | bytes 3932160 | tf_op jit(solution)/shard_map/all_gather | solution.py:21
  124.8 10.9 %copy-start.1 = (f32[2048,1024]{1,0:T(8,128)S(1)}, f32[2048,1024]{1,0:T(8,128)}, u32[]{:S(2)}) copy-start(f32[2048,1024]{1,0:T(8,128)} %get-tuple-element.292) | copy-start | bytes 25165828 | tf_op jit(solution)/shard_map/while
  147.0 6.5 copy-start.3
  162.9 12.4 %copy-start.1 = (f32[2048,1024]{1,0:T(8,128)S(1)}, f32[2048,1024]{1,0:T(8,128)}, u32[]{:S(2)}) copy-start(f32[2048,1024]{1,0:T(8,128)} %get-tuple-element.292) | copy-start | bytes 25165828 | tf_op jit(solution)/shard_map/while
  190.1 6.5 copy-start.3
  206.0 12.4 %copy-start.1 = (f32[2048,1024]{1,0:T(8,128)S(1)}, f32[2048,1024]{1,0:T(8,128)}, u32[]{:S(2)}) copy-start(f32[2048,1024]{1,0:T(8,128)} %get-tuple-element.292) | copy-start | bytes 25165828 | tf_op jit(solution)/shard_map/while
  233.2 6.5 copy-start.3
  249.1 12.4 %copy-start.1 = (f32[2048,1024]{1,0:T(8,128)S(1)}, f32[2048,1024]{1,0:T(8,128)}, u32[]{:S(2)}) copy-start(f32[2048,1024]{1,0:T(8,128)} %get-tuple-element.292) | copy-start | bytes 25165828 | tf_op jit(solution)/shard_map/while
  276.4 6.5 copy-start.3
  292.2 12.4 %copy-start.1 = (f32[2048,1024]{1,0:T(8,128)S(1)}, f32[2048,1024]{1,0:T(8,128)}, u32[]{:S(2)}) copy-start(f32[2048,1024]{1,0:T(8,128)} %get-tuple-element.292) | copy-start | bytes 25165828 | tf_op jit(solution)/shard_map/while
  319.5 6.5 copy-start.3
  335.3 12.4 %copy-start.1 = (f32[2048,1024]{1,0:T(8,128)S(1)}, f32[2048,1024]{1,0:T(8,128)}, u32[]{:S(2)}) copy-start(f32[2048,1024]{1,0:T(8,128)} %get-tuple-element.292) | copy-start | bytes 25165828 | tf_op jit(solution)/shard_map/while
  362.6 6.5 copy-start.3
  378.5 12.4 %copy-start.1 = (f32[2048,1024]{1,0:T(8,128)S(1)}, f32[2048,1024]{1,0:T(8,128)}, u32[]{:S(2)}) copy-start(f32[2048,1024]{1,0:T(8,128)} %get-tuple-element.292) | copy-start | bytes 25165828 | tf_op jit(solution)/shard_map/while
  405.7 6.5 copy-start.3
  421.6 12.4 %copy-start.1 = (f32[2048,1024]{1,0:T(8,128)S(1)}, f32[2048,1024]{1,0:T(8,128)}, u32[]{:S(2)}) copy-start(f32[2048,1024]{1,0:T(8,128)} %get-tuple-element.292) | copy-start | bytes 25165828 | tf_op jit(solution)/shard_map/while
  464.7 12.4 %copy-start.1 = (f32[2048,1024]{1,0:T(8,128)S(1)}, f32[2048,1024]{1,0:T(8,128)}, u32[]{:S(2)}) copy-start(f32[2048,1024]{1,0:T(8,128)} %get-tuple-element.292) | copy-start | bytes 25165828 | tf_op jit(solution)/shard_map/while
  507.8 12.4 %copy-start.1 = (f32[2048,1024]{1,0:T(8,128)S(1)}, f32[2048,1024]{1,0:T(8,128)}, u32[]{:S(2)}) copy-start(f32[2048,1024]{1,0:T(8,128)} %get-tuple-element.292) | copy-start | bytes 25165828 | tf_op jit(solution)/shard_map/while
  550.9 12.4 %copy-start.1 = (f32[2048,1024]{1,0:T(8,128)S(1)}, f32[2048,1024]{1,0:T(8,128)}, u32[]{:S(2)}) copy-start(f32[2048,1024]{1,0:T(8,128)} %get-tuple-element.292) | copy-start | bytes 25165828 | tf_op jit(solution)/shard_map/while
  594.1 12.4 %copy-start.1 = (f32[2048,1024]{1,0:T(8,128)S(1)}, f32[2048,1024]{1,0:T(8,128)}, u32[]{:S(2)}) copy-start(f32[2048,1024]{1,0:T(8,128)} %get-tuple-element.292) | copy-start | bytes 25165828 | tf_op jit(solution)/shard_map/while
  637.2 12.4 %copy-start.1 = (f32[2048,1024]{1,0:T(8,128)S(1)}, f32[2048,1024]{1,0:T(8,128)}, u32[]{:S(2)}) copy-start(f32[2048,1024]{1,0:T(8,128)} %get-tuple-element.292) | copy-start | bytes 25165828 | tf_op jit(solution)/shard_map/while
  680.3 12.4 %copy-start.1 = (f32[2048,1024]{1,0:T(8,128)S(1)}, f32[2048,1024]{1,0:T(8,128)}, u32[]{:S(2)}) copy-start(f32[2048,1024]{1,0:T(8,128)} %get-tuple-element.292) | copy-start | bytes 25165828 | tf_op jit(solution)/shard_map/while
  723.4 12.4 %copy-start.1 = (f32[2048,1024]{1,0:T(8,128)S(1)}, f32[2048,1024]{1,0:T(8,128)}, u32[]{:S(2)}) copy-start(f32[2048,1024]{1,0:T(8,128)} %get-tuple-element.292) | copy-start | bytes 25165828 | tf_op jit(solution)/shard_map/while
  766.5 12.4 %copy-start.1 = (f32[2048,1024]{1,0:T(8,128)S(1)}, f32[2048,1024]{1,0:T(8,128)}, u32[]{:S(2)}) copy-start(f32[2048,1024]{1,0:T(8,128)} %get-tuple-element.292) | copy-start | bytes 25165828 | tf_op jit(solution)/shard_map/while
  (26 other events, 142.9 us)
Sparse Core Ops, SparseCore 0:
  94.8 27.5 all-gather.1
where the time goes:
time: 856 us; the launch traced here: 855 us
  other arithmetic  436 us (51%)
  matrix products  131 us (15%)
  local copies, waits for them, and re-layouts  124 us (14%)
  blocking collectives  123 us (14%)
  waiting for transfers between devices  16.7 us (2%)
  between operations  14.1 us (2%)
  loops' own time  10.5 us (1%)
    another operation x32, other arithmetic, advance(): stacked = jnp.stack(term_list)  431 us
    dot_general x16, matrix products, advance(): jnp.einsum('grc,cm->grm', stacked, filtered_cols, preferred_element_type=...  127 us
    while x112, local copies, waits for them, and re-layouts  104 us
    psum x1, blocking collectives, per_device(): filtered = lax.psum(partial_value, 'pcol').astype(jnp.bfloat16)  82.8 us
    psum x1, blocking collectives, per_device(): spectra = lax.psum(partial_spectra.reshape(L, -1), ('prow', 'pcol'))  40.1 us
  transfers between devices with their start and end apart: 1, of which 1 were waited for; matrix products, arithmetic and copies ran while one was open for 1% of the time, Pallas kernels for 0%

commit v1 on v0

v1 whole, which is shorter than its diff:
```python
import functools
import math
import random

import jax
import jax.numpy as jnp
import numpy as np
from jax import lax
from jax.experimental import pallas as pl
from jax.experimental.pallas import tpu as pltpu
from jax.sharding import PartitionSpec as P

L = 64
LMIN = 2
TILE = 256
STRIP = 16
GROUP = 11
CHUNKS = 6
LEVELS = GROUP * CHUNKS


def transform_matrix(npix):
    top = LMIN + L - 1
    a = [math.comb(2 * k, k) / 4.0**k for k in range(top + 1)]
    out = np.zeros((L, LEVELS + 1))
    for l in range(LMIN, top + 1):
        for k in range(l + 1):
            degree = abs(l - 2 * k)
            column = degree - 1 if degree else LEVELS
            out[l - LMIN, column] += a[k] * a[l - k]
        out[l - LMIN] *= (2 * l + 1) / npix
    return out.astype(np.float32)


def pair_up(tiles, n):
    items = []
    for col in range(n):
        mine = sorted((t for t in tiles if t[1] == col), key=lambda t: t[0])
        for k in range(0, len(mine), 2):
            first = mine[k]
            second = mine[k + 1] if k + 1 < len(mine) else (first[0], col, 0)
            items.append((first[0], second[0], first[2], second[2], col))
    return items


def work_tables(n):
    lower = [[(h * n + i, j, 2) for i in range(n) for j in range(n)] for h in range(2)]
    rng = random.Random(0)
    best = None
    for _ in range(20000):
        sets = []
        cross = [[rng.random() < 0.5 for _ in range(n)] for _ in range(n)]
        for h in range(2):
            tiles = []
            for i in range(n):
                tiles.append((h * n + i, i, 1))
                for j in range(i):
                    a, b = (i, j) if rng.random() < 0.5 else (j, i)
                    tiles.append((h * n + a, b, 2))
                for j in range(n):
                    if h == 0 and cross[i][j]:
                        tiles.append((n + i, j, 2))
                    if h == 1 and not cross[i][j]:
                        tiles.append((j, i, 2))
            sets.append(pair_up(tiles, n))
        cost = max(len(s) for s in sets)
        if best is None or cost < best[0]:
            best = (cost, sets)
        if 2 * cost <= n * n + n // 2 + 1:
            break
    kinds = [pair_up(lower[0], n), pair_up(lower[1], n), pair_up(lower[1], n), pair_up(lower[0], n)] + best[1]
    longest = max(len(k) for k in kinds)
    table = np.zeros((len(kinds), longest + 1, 5), np.int32)
    for k, items in enumerate(kinds):
        table[k, : len(items)] = items
    counts = np.array([len(k) for k in kinds], np.int32)
    return table.reshape(-1), counts, longest + 1


def moments_kernel(
    stride, table, counts, cos_hbm, ft, fct, out,
    xbuf, x2, prev, cur, buf_a, buf_b, lhs, fj, acc, sem,
):
    r = lax.axis_index("prow")
    c = lax.axis_index("pcol")
    q, h = c // 2, c % 2
    kind = jnp.where(r > q, h, jnp.where(r < q, 2 + h, 4 + h))
    n_items = counts[kind]

    def field(item, f):
        return table[(kind * stride + item) * 5 + f]

    def tile_copy(item, half):
        row = pl.multiple_of(field(item, half) * TILE, TILE)
        col = pl.multiple_of(field(item, 4) * TILE, TILE)
        return pltpu.make_async_copy(
            cos_hbm.at[pl.ds(row, TILE), pl.ds(col, TILE)],
            xbuf.at[pl.ds(half * TILE, TILE)],
            sem.at[half],
        )

    def fetch(item):
        tile_copy(item, 0).start()
        tile_copy(item, 1).start()

    def begin(item):
        tile_copy(item, 0).wait()
        tile_copy(item, 1).wait()
        x = xbuf[...]
        x2[...] = x + x
        prev[...] = x
        cur[...] = jnp.ones_like(x)

    def set_operands(item):
        col = pl.multiple_of(field(item, 4) * TILE, TILE)
        for half in range(2):
            row = pl.multiple_of(field(item, half) * TILE, TILE)
            weight = field(item, 2 + half).astype(jnp.float32)
            value = ft[:, pl.ds(row, TILE)].astype(jnp.float32) * weight
            lhs[:, half * TILE : (half + 1) * TILE] = value.astype(jnp.bfloat16)
        fj[...] = fct[:, pl.ds(col, TILE)].astype(jnp.float32)

    n_strips = 2 * TILE // STRIP

    def gen_strip(buf, s):
        rows = pl.ds(s * STRIP, STRIP)
        xx = x2[rows, :]
        p = prev[rows, :]
        t = cur[rows, :]
        for g in range(GROUP):
            p, t = t, xx * t - p
            buf[g, rows, :] = t.astype(jnp.bfloat16)
        prev[rows, :] = p
        cur[rows, :] = t

    def half_step(gen, use, level0):
        done = 0
        for g in range(GROUP):
            upto = (g + 1) * n_strips // GROUP
            for s in range(done, upto):
                gen_strip(gen, s)
            done = upto
            image = jnp.dot(lhs[...], use[g], preferred_element_type=jnp.float32)
            prod = image * fj[...]
            half_tile = TILE // 2
            acc[level0 + g] += prod[:, :half_tile] + prod[:, half_tile:]

    acc[...] = jnp.zeros_like(acc)
    fetch(0)
    begin(0)
    for s in range(n_strips):
        gen_strip(buf_a, s)

    def item_loop(item, carry):
        fetch(item + 1)
        set_operands(item)

        def chunk_loop(cp, carry):
            half_step(buf_b, buf_a, cp * 2 * GROUP)

            @pl.when(cp == CHUNKS // 2 - 1)
            def _():
                begin(item + 1)

            half_step(buf_a, buf_b, cp * 2 * GROUP + GROUP)
            return carry

        return lax.fori_loop(0, CHUNKS // 2, chunk_loop, carry)

    lax.fori_loop(0, n_items, item_loop, 0)
    out[...] = jnp.sum(acc[...], axis=-1)


def spectra_moments(cosines, ft, fct):
    maps = ft.shape[0]
    n = cosines.shape[1] // TILE
    table, counts, stride = work_tables(n)
    vmem = pl.BlockSpec(memory_space=pltpu.VMEM)
    smem = pl.BlockSpec(memory_space=pltpu.SMEM)
    return pl.pallas_call(
        functools.partial(moments_kernel, stride),
        out_shape=jax.ShapeDtypeStruct((LEVELS, maps), jnp.float32),
        in_specs=[smem, smem, pl.BlockSpec(memory_space=pl.ANY), vmem, vmem],
        out_specs=vmem,
        scratch_shapes=[
            pltpu.VMEM((2 * TILE, TILE), jnp.float32),
            pltpu.VMEM((2 * TILE, TILE), jnp.float32),
            pltpu.VMEM((2 * TILE, TILE), jnp.float32),
            pltpu.VMEM((2 * TILE, TILE), jnp.float32),
            pltpu.VMEM((GROUP, 2 * TILE, TILE), jnp.bfloat16),
            pltpu.VMEM((GROUP, 2 * TILE, TILE), jnp.bfloat16),
            pltpu.VMEM((maps, 2 * TILE), jnp.bfloat16),
            pltpu.VMEM((maps, TILE), jnp.float32),
            pltpu.VMEM((LEVELS, maps, TILE // 2), jnp.float32),
            pltpu.SemaphoreType.DMA((2,)),
        ],
        compiler_params=pltpu.CompilerParams(vmem_limit_bytes=48 * 2**20),
        name="moments",
    )(jnp.asarray(table), jnp.asarray(counts), cosines, ft, fct)


def per_device(npix, inverse_cov, cosines, sky_maps):
    cols_here = inverse_cov.shape[1]
    partial_value = jnp.dot(inverse_cov, sky_maps, preferred_element_type=jnp.float32)
    filtered = lax.psum(partial_value, "pcol").astype(jnp.bfloat16)
    column_index = lax.axis_index("pcol")
    full_maps = lax.all_gather(filtered, "prow", axis=0, tiled=True)
    filtered_cols = lax.dynamic_slice_in_dim(full_maps, column_index * cols_here, cols_here, 0)
    moments = spectra_moments(cosines, filtered.T, filtered_cols.T)
    row_sum = jnp.sum(filtered.astype(jnp.float32), axis=0)
    col_sum = jnp.sum(filtered_cols.astype(jnp.float32), axis=0)
    moments = jnp.concatenate([moments, (row_sum * col_sum)[None]], axis=0)
    matrix = jnp.asarray(transform_matrix(npix))
    partial_spectra = jnp.dot(matrix, moments, precision=lax.Precision.HIGHEST)
    spectra = lax.psum(partial_spectra, ("prow", "pcol"))
    return (filtered, spectra)


def solution(mesh):
    in_specs = (P("prow", "pcol"), P("prow", "pcol"), P("pcol", None))
    out_specs = (P("prow", None), P())

    def whole(inverse_cov, cosines, sky_maps):
        npix = cosines.shape[0]
        step = jax.shard_map(
            functools.partial(per_device, npix),
            mesh=mesh, in_specs=in_specs, out_specs=out_specs, check_vma=False,
        )
        return step(inverse_cov, cosines, sky_maps)

    return whole
```

time: 856 us -> 229 us (0.27)
  other arithmetic: 436 us -> 2.52 us
  matrix products: 131 us -> 3.91 us
  local copies, waits for them, and re-layouts: 124 us -> 2.01 us
  Pallas kernels: 0 us -> 56.6 us
  loops' own time: 10.5 us -> 0 us
  waiting for transfers between devices: 16.7 us -> 26.3 us
    another operation x48 -> x0, other arithmetic: 432 us -> none  [the longest x32 431 us: advance(): stacked = jnp.stack(term_list)]
    dot_general x16 -> x1, matrix products: 127 us -> 0.2 us  [per_device(): partial_spectra = jnp.dot(matrix, moments, precision=lax.Precision.HIGHEST)]
    while x112 -> x0, local copies, waits for them, and re-layouts: 104 us -> none
    pallas_call x0 -> x1, Pallas kernels: none -> 56.6 us  [spectra_moments(): pl.pallas_call(functools.partial(moments_kernel, stride), out_shape=jax.S...]
    dynamic_slice x17 -> x0, local copies, waits for them, and re-layouts: 10.9 us -> none  [the longest x16 9.87 us: per_device(): lax.scan(advance, (previous, current), jnp.arange(L // GROUP, dtype=jnp.i...]
    another operation x1 -> x0, loops' own time: 10.5 us -> none  [per_device(): lax.scan(advance, (previous, current), jnp.arange(L // GROUP, dtype=jnp.i...]
    all_gather x1, waiting for transfers between devices: 16.7 us -> 26.3 us  [per_device(): full_maps = lax.all_gather(filtered, 'prow', axis=0, tiled=True)]
where the time goes in v1:
time: 229 us; the launch traced here: 228 us
  blocking collectives  123 us (54%)
  Pallas kernels  56.6 us (25%)
  waiting for transfers between devices  26.3 us (11%)
  between operations  14.1 us (6%)
  matrix products  3.91 us (2%)
  other arithmetic  2.52 us (1%)
    psum x1, blocking collectives, per_device(): filtered = lax.psum(partial_value, 'pcol').astype(jnp.bfloat16)  82.8 us
    pallas_call x1, Pallas kernels, spectra_moments(): pl.pallas_call(functools.partial(moments_kernel, stride), out_shape=jax.S...  56.6 us
    psum x1, blocking collectives, per_device(): spectra = lax.psum(partial_spectra, ('prow', 'pcol'))  40 us
    all_gather x1, waiting for transfers between devices, per_device(): full_maps = lax.all_gather(filtered, 'prow', axis=0, tiled=True)  26.3 us
  transfers between devices with their start and end apart: 1, of which 1 were waited for; matrix products, arithmetic and copies ran while one was open for 1% of the time, Pallas kernels for 0%

profile of v1, /device:TPU:0, one launch (start us, length us, event | category | flops | bytes accessed | tf_op | source)
XLA Modules:
  0.0 228.4 jit_solution(6183366306254110210)
XLA Ops:
  7.2 0.0 copy-start
  7.2 0.0 all-gather.2.cloned.1.call-start
  7.2 0.9 copy-done
  8.2 3.7 %fusion.1 = f32[2048,192]{0,1:T(8,128)S(1)} fusion(bf16[2048,1024]{1,0:T(8,128)(2,1)} %param.6, bf16[1024,192]{0,1:T(8,128)(2,1)S(1)} %copy-done), kind=kOutput, calls=%fused_computation.5 | convolution fusion | flops 805306368 | bytes 6160384 | tf_op jit(solution)/shard_map/dot_general | solution.py:204
  11.9 0.0 copy-start.2
  11.9 0.0 copy-start.3
  11.9 82.8 %all-reduce.1 = bf16[2048,192]{0,1:T(8,128)(2,1)} all-reduce(f32[2048,192]{0,1:T(8,128)S(1)} %fusion.1), channel_id=1, replica_groups=mesh['prow'=4,'pcol'=8] {'pcol'}, use_global_device_ids=true, to_apply=%region_0.0 | all-reduce | flops 393216 | bytes 2359296 | tf_op jit(solution)/shard_map/psum | solution.py:205
  94.7 0.0 copy-start.1
  94.7 0.0 all-gather.2.cloned.1.call-update
  94.7 1.4 convert_reduce_fusion
  96.1 26.3 %all-gather.2.cloned.1.call-done = bf16[8192,192]{0,1:T(8,128)(2,1)} async-done(((bf16[2048,192]{0,1:T(8,128)(2,1)}), bf16[8192,192]{0,1:T(8,128)(2,1)}) %all-gather.2.cloned.1.call-update) | async-done | bytes 3145744 | tf_op jit(solution)/shard_map/all_gather | solution.py:207
  122.4 1.1 convert_reduce_fusion.1
  123.6 1.0 dynamic-slice_bitcast_fusion.fct
  124.6 0.0 copy-done.2
  124.6 0.0 copy-done.3
  124.6 0.0 copy-done.1
  124.6 0.0 copy-start.4
  124.7 0.0 copy-start.5
  124.7 56.6 %moments.1 = f32[66,192]{1,0:T(8,128)S(1)} custom-call(s32[300]{0:T(512)S(1)} %copy-done.2, s32[6]{0:T(128)S(1)} %copy-done.3, f32[2048,1024]{1,0:T(8,128)} %cos_hbm.1, bf16[192,2048]{1,0:T(8,128)(2,1)S(1)} %bitcast.9, bf16[192,1024]{1,0:T(8,128)(2,1)S(1)} %dynamic-slice_bitcast_fusion.fct), custom_call_target="tpu_custom_call" | custom-call | tf_op jit(solution)/shard_map/moments/pallas_call | solution.py:180
  181.3 0.0 copy-done.4
  181.3 0.0 copy-done.5
  181.3 0.2 fusion
  181.5 40.0 %psum.15 = f32[64,192]{1,0:T(8,128)} all-reduce(f32[64,192]{1,0:T(8,128)S(1)} %fusion), channel_id=1, replica_groups=mesh['prow'=4,'pcol'=8] {'prow','pcol'}, use_global_device_ids=true, to_apply=%region_3.0 | all-reduce | flops 12288 | bytes 98304 | tf_op jit(solution)/shard_map/psum | solution.py:215
  (1 shorter events, 0.0 us)
Async XLA Ops:
  7.2 1.0 copy-start
  7.2 115.3 %all-gather.2.cloned.1.call-start = ((), (), s32[]{:S(2)}) async-start(), calls=%async_computation | async-start | bytes 3932160 | tf_op jit(solution)/shard_map/all_gather | solution.py:207
  11.9 112.7 %copy-start.2 = (s32[300]{0:T(512)S(1)}, s32[300]{0:T(512)}, u32[]{:S(2)}) copy-start(s32[300]{0:T(512)} %constant.18.clone.table) | copy-start | bytes 3604
  11.9 112.7 %copy-start.3 = (s32[6]{0:T(128)S(1)}, s32[6]{0:T(128)}, u32[]{:S(2)}) copy-start(s32[6]{0:T(128)} %constant.19.clone.counts) | copy-start | bytes 76
  94.7 29.9 %copy-start.1 = (bf16[2048,192]{0,1:T(8,128)(2,1)S(1)}, bf16[2048,192]{0,1:T(8,128)(2,1)}, u32[]{:S(2)}) copy-start(bf16[2048,192]{0,1:T(8,128)(2,1)} %all-reduce.1) | copy-start | bytes 2359300
  124.6 56.6 %copy-start.4 = (f32[64,66]{1,0:T(8,128)S(1)}, f32[64,66]{1,0:T(8,128)}, u32[]{:S(2)}) copy-start(f32[64,66]{1,0:T(8,128)} %constant.21) | copy-start | bytes 50692
  124.7 56.6 %copy-start.5 = (f32[64]{0:T(128)S(1)}, f32[64]{0:T(128)}, u32[]{:S(2)}) copy-start(f32[64]{0:T(128)} %constant.23) | copy-start | bytes 772
Sparse Core Ops, SparseCore 0:
  94.9 27.5 all-gather.1

commit v2 on v1

--- a/solution.py
+++ b/solution.py
@@ -19,17 +19,18 @@
 LEVELS = GROUP * CHUNKS
 
 
-def transform_matrix(npix):
+def transform_matrix(npix, devices):
     top = LMIN + L - 1
+    each = -(-L // devices)
     a = [math.comb(2 * k, k) / 4.0**k for k in range(top + 1)]
-    out = np.zeros((L, LEVELS + 1))
+    out = np.zeros((devices * 8, LEVELS))
     for l in range(LMIN, top + 1):
+        owner, place = divmod(l - LMIN, each)
+        row = out[owner * 8 + place]
         for k in range(l + 1):
-            degree = abs(l - 2 * k)
-            column = degree - 1 if degree else LEVELS
-            out[l - LMIN, column] += a[k] * a[l - k]
-        out[l - LMIN] *= (2 * l + 1) / npix
-    return out.astype(np.float32)
+            row[abs(l - 2 * k)] += a[k] * a[l - k]
+        row *= (2 * l + 1) / npix
+    return out.astype(np.float32), each
 
 
 def pair_up(tiles, n):
@@ -108,8 +109,8 @@
         tile_copy(item, 1).wait()
         x = xbuf[...]
         x2[...] = x + x
-        prev[...] = x
-        cur[...] = jnp.ones_like(x)
+        prev[...] = (x + x) * x - 1.0
+        cur[...] = x
 
     def set_operands(item):
         col = pl.multiple_of(field(item, 4) * TILE, TILE)
@@ -199,31 +200,218 @@
     )(jnp.asarray(table), jnp.asarray(counts), cosines, ft, fct)
 
 
-def per_device(npix, inverse_cov, cosines, sky_maps):
+MESH = pl.DeviceIdType.MESH
+
+
+def spread_kernel(n_q, block, out, far_send, near_send, far_recv, side_send, side_recv):
+    r = lax.axis_index("prow")
+    c = lax.axis_index("pcol")
+    q, h = c // 2, c % 2
+    width = block.shape[1]
+    pieces = far_recv.shape[0]
+    step = width // pieces
+    partner = (r, c + 1 - 2 * h)
+    above, below = (r, c + 2), (r, c - 2)
+    has_above, has_below = q < n_q - 1, q > 0
+    barrier = pltpu.get_barrier_semaphore()
+    pl.semaphore_signal(barrier, inc=1, device_id=partner, device_id_type=MESH)
+
+    @pl.when(has_above)
+    def _():
+        pl.semaphore_signal(barrier, inc=1, device_id=above, device_id_type=MESH)
+
+    @pl.when(has_below)
+    def _():
+        pl.semaphore_signal(barrier, inc=1, device_id=below, device_id_type=MESH)
+
+    pl.semaphore_wait(barrier, 1 + has_above.astype(jnp.int32) + has_below.astype(jnp.int32))
+
+    source = q == r
+    up = jnp.logical_and(q >= r, has_above)
+    down = jnp.logical_and(q <= r, has_below)
+
+    def columns(half, k):
+        return pl.ds(pl.multiple_of(half * width + k * step, 128), step)
+
+    def remote(src, k, send, recv, device):
+        return pltpu.make_async_remote_copy(
+            src_ref=src,
+            dst_ref=out.at[:, columns(h, k)],
+            send_sem=send.at[k],
+            recv_sem=recv.at[k],
+            device_id=device,
+            device_id_type=MESH,
+        )
+
+    def send_all(src, k):
+        @pl.when(up)
+        def _():
+            remote(src, k, far_send, far_recv, above).start()
+
+        @pl.when(down)
+        def _():
+            remote(src, k, near_send, far_recv, below).start()
+
+        remote(src, k, side_send, side_recv, partner).start()
+
+    @pl.when(source)
+    def _():
+        for k in range(pieces):
+            send_all(block.at[:, pl.ds(k * step, step)], k)
+        out[:, pl.ds(pl.multiple_of(h * width, 128), width)] = block[...]
+
+    @pl.when(jnp.logical_not(source))
+    def _():
+        for k in range(pieces):
+            landed = out.at[:, columns(h, k)]
+            remote(landed, k, side_send, far_recv, partner).wait_recv()
+            send_all(landed, k)
+
+    for k in range(pieces):
+        mine = block.at[:, pl.ds(k * step, step)]
+
+        @pl.when(up)
+        def _():
+            remote(mine, k, far_send, far_recv, above).wait_send()
+
+        @pl.when(down)
+        def _():
+            remote(mine, k, near_send, far_recv, below).wait_send()
+
+        remote(mine, k, side_send, side_recv, partner).wait_send()
+        pltpu.make_async_remote_copy(
+            src_ref=mine,
+            dst_ref=out.at[:, columns(1 - h, k)],
+            send_sem=side_send.at[k],
+            recv_sem=side_recv.at[k],
+            device_id=partner,
+            device_id_type=MESH,
+        ).wait_recv()
+
+
+def spread(block, n_q, collective_id):
+    maps, width = block.shape
+    pieces = min(4, width // 128)
+    vmem = pl.BlockSpec(memory_space=pltpu.VMEM)
+    sems = pltpu.SemaphoreType.DMA((pieces,))
+    return pl.pallas_call(
+        functools.partial(spread_kernel, n_q),
+        out_shape=jax.ShapeDtypeStruct((maps, 2 * width), block.dtype),
+        in_specs=[vmem],
+        out_specs=vmem,
+        scratch_shapes=[sems] * 5,
+        compiler_params=pltpu.CompilerParams(
+            collective_id=collective_id, has_side_effects=True
+        ),
+        name="spread%d" % collective_id,
+    )(block)
+
+
+def sum_kernel(n, place_of, device_of, x, out, landed, result, send1, recv1, send2, recv2):
+    me = place_of()
+    barrier = pltpu.get_barrier_semaphore()
+
+    def each(body):
+        lax.fori_loop(1, n, lambda k, carry: (body(k), carry)[1], 0)
+
+    def member(k):
+        return device_of(lax.rem(me + k, n))
+
+    each(lambda k: pl.semaphore_signal(barrier, inc=1, device_id=member(k), device_id_type=MESH))
+    pl.semaphore_wait(barrier, n - 1)
+
+    def scatter(k):
+        return pltpu.make_async_remote_copy(
+            src_ref=x.at[lax.rem(me + k, n)],
+            dst_ref=landed.at[k - 1],
+            send_sem=send1.at[k - 1],
+            recv_sem=recv1.at[k - 1],
+            device_id=member(k),
+            device_id_type=MESH,
+        )
+
+    def gather(k, slot):
+        return pltpu.make_async_remote_copy(
+            src_ref=result,
+            dst_ref=out.at[slot],
+            send_sem=send2.at[k - 1],
+            recv_sem=recv2.at[k - 1],
+            device_id=member(k),
+            device_id_type=MESH,
+        )
+
+    each(lambda k: scatter(k).start())
+    each(lambda k: scatter(k).wait_recv())
+    total = lax.fori_loop(0, n - 1, lambda k, t: t + landed[k], x[me]) if n > 8 else sum(
+        (landed[k] for k in range(n - 1)), x[me]
+    )
+    result[...] = total.astype(result.dtype)
+    each(lambda k: gather(k, me).start())
+    out[me] = result[...]
+    each(lambda k: gather(k, lax.rem(me - k + n, n)).wait_recv())
+    each(lambda k: scatter(k).wait_send())
+    each(lambda k: gather(k, me).wait_send())
+
+
+def sum_and_share(x, dtype, place_of, device_of, collective_id):
+    n, rows, cols = x.shape
+    vmem = pl.BlockSpec(memory_space=pltpu.VMEM)
+    sems = pltpu.SemaphoreType.DMA((n - 1,))
+    return pl.pallas_call(
+        functools.partial(sum_kernel, n, place_of, device_of),
+        out_shape=jax.ShapeDtypeStruct(x.shape, dtype),
+        in_specs=[vmem],
+        out_specs=vmem,
+        scratch_shapes=[
+            pltpu.VMEM((n - 1, rows, cols), x.dtype),
+            pltpu.VMEM((rows, cols), dtype),
+            sems, sems, sems, sems,
+        ],
+        compiler_params=pltpu.CompilerParams(
+            collective_id=collective_id, has_side_effects=True
+        ),
+        name="sum%d" % collective_id,
+    )(x)
+
+
+def per_device(npix, n_rows, n_cols, inverse_cov, cosines, sky_maps):
+    maps = sky_maps.shape[1]
     cols_here = inverse_cov.shape[1]
-    partial_value = jnp.dot(inverse_cov, sky_maps, preferred_element_type=jnp.float32)
-    filtered = lax.psum(partial_value, "pcol").astype(jnp.bfloat16)
-    column_index = lax.axis_index("pcol")
-    full_maps = lax.all_gather(filtered, "prow", axis=0, tiled=True)
-    filtered_cols = lax.dynamic_slice_in_dim(full_maps, column_index * cols_here, cols_here, 0)
-    moments = spectra_moments(cosines, filtered.T, filtered_cols.T)
-    row_sum = jnp.sum(filtered.astype(jnp.float32), axis=0)
-    col_sum = jnp.sum(filtered_cols.astype(jnp.float32), axis=0)
-    moments = jnp.concatenate([moments, (row_sum * col_sum)[None]], axis=0)
-    matrix = jnp.asarray(transform_matrix(npix))
-    partial_spectra = jnp.dot(matrix, moments, precision=lax.Precision.HIGHEST)
-    spectra = lax.psum(partial_spectra, ("prow", "pcol"))
-    return (filtered, spectra)
+    n_q = n_cols // 2
+    sky_rows = spread(sky_maps.T, n_q, 1)
+    partial_value = jnp.dot(sky_rows, inverse_cov, preferred_element_type=jnp.float32)
+    column_maps = sum_and_share(
+        partial_value.reshape(n_rows, maps // n_rows, cols_here),
+        jnp.bfloat16,
+        lambda: lax.axis_index("prow"),
+        lambda i: (i, lax.axis_index("pcol")),
+        2,
+    ).reshape(maps, cols_here)
+    row_maps = spread(column_maps, n_q, 3)
+    moments = spectra_moments(cosines, row_maps, column_maps)
+    devices = n_rows * n_cols
+    matrix, each = transform_matrix(npix, devices)
+    partial_spectra = jnp.dot(jnp.asarray(matrix), moments, precision=lax.Precision.HIGHEST)
+    shared = sum_and_share(
+        partial_spectra.reshape(devices, 8, maps),
+        jnp.float32,
+        lambda: lax.axis_index("prow") * n_cols + lax.axis_index("pcol"),
+        lambda i: (i // n_cols, lax.rem(i, n_cols)),
+        4,
+    )
+    spectra = shared[:, :each].reshape(devices * each, maps)[:L]
+    return (row_maps.T, spectra)
 
 
 def solution(mesh):
     in_specs = (P("prow", "pcol"), P("prow", "pcol"), P("pcol", None))
     out_specs = (P("prow", None), P())
+    n_rows, n_cols = mesh.shape["prow"], mesh.shape["pcol"]
 
     def whole(inverse_cov, cosines, sky_maps):
         npix = cosines.shape[0]
         step = jax.shard_map(
-            functools.partial(per_device, npix),
+            functools.partial(per_device, npix, n_rows, n_cols),
             mesh=mesh, in_specs=in_specs, out_specs=out_specs, check_vma=False,
         )
         return step(inverse_cov, cosines, sky_maps)

time: 229 us -> 146 us (0.64)
  blocking collectives: 123 us -> 0 us
  Pallas kernels: 56.6 us -> 135 us
  waiting for transfers between devices: 26.3 us -> 0 us
  between operations: 14.1 us -> 0.72 us
  local copies, waits for them, and re-layouts: 2.01 us -> 4.67 us
  other arithmetic: 2.52 us -> 0 us
    psum x2 -> x0, blocking collectives: 123 us -> none  [the longest x1 82.8 us: per_device(): filtered = lax.psum(partial_value, 'pcol').astype(jnp.bfloat16)]
    pallas_call x0 -> x4, Pallas kernels: none -> 81.3 us  [the longest x2 55.1 us: sum_and_share(): pl.pallas_call(functools.partial(sum_kernel, n, place_of, device_of), out...]
    all_gather x1 -> x0, waiting for transfers between devices: 26.3 us -> none  [per_device(): full_maps = lax.all_gather(filtered, 'prow', axis=0, tiled=True)]
    pallas_call x1, Pallas kernels: 56.6 us -> 53.8 us  [spectra_moments(): pl.pallas_call(functools.partial(moments_kernel, stride), out_shape=jax.S...]
    reduce_sum x2 -> x0, other arithmetic: 2.51 us -> none  [the longest x1 1.39 us: per_device(): row_sum = jnp.sum(filtered.astype(jnp.float32), axis=0)]
  transfers between devices with their start and end apart: 1 -> 0, of which waited for: 1 -> 0; matrix products, arithmetic and copies ran while one was open for 1% -> 0% of each run, Pallas kernels for 0% -> 0%
where the time goes in v2:
time: 146 us
  Pallas kernels  135 us (92%)
  matrix products  5.37 us (4%)
  local copies, waits for them, and re-layouts  4.67 us (3%)
    pallas_call x2, Pallas kernels, sum_and_share(): pl.pallas_call(functools.partial(sum_kernel, n, place_of, device_of), out...  55.1 us
    pallas_call x1, Pallas kernels, spectra_moments(): pl.pallas_call(functools.partial(moments_kernel, stride), out_shape=jax.S...  53.8 us
    pallas_call x2, Pallas kernels, spread(): pl.pallas_call(functools.partial(spread_kernel, n_q), out_shape=jax.Shape...  26.1 us
    dot_general x1, matrix products, per_device(): jnp.dot(sky_rows, inverse_cov, preferred_element_type=jnp.float32)  4.31 us
    unnamed x13, local copies, waits for them, and re-layouts  3.02 us

profile of v2, /device:TPU:0, one launch (start us, length us, event | category | flops | bytes accessed | tf_op | source)
XLA Modules:
  0.0 145.8 jit_solution(11679205173084304820)
XLA Ops:
  0.6 14.1 %spread1.1 = bf16[192,2048]{1,0:T(8,128)(2,1)} custom-call(bf16[192,1024]{1,0:T(8,128)(2,1)} %bitcast.14), custom_call_target="tpu_custom_call" | custom-call | tf_op jit(solution)/shard_map/spread1/pallas_call | solution.py:297
  14.8 0.0 copy-start.3
  14.8 0.0 copy-start.4
  14.8 4.3 %fusion = f32[192,1024]{1,0:T(8,128)} fusion(bf16[192,2048]{1,0:T(8,128)(2,1)} %spread1.1, bf16[2048,1024]{1,0:T(8,128)(2,1)} %param.6), kind=kOutput, calls=%fused_computation.1 | convolution fusion | flops 805306368 | bytes 5767168 | tf_op jit(solution)/shard_map/dot_general | solution.py:382
  19.1 28.2 %sum2.1 = bf16[4,48,1024]{2,1,0:T(8,128)(2,1)} custom-call(f32[4,48,1024]{2,1,0:T(8,128)} %bitcast.13), custom_call_target="tpu_custom_call" | custom-call | tf_op jit(solution)/shard_map/sum2/pallas_call | solution.py:360
  47.3 12.0 %spread3.1.ft = bf16[192,2048]{1,0:T(8,128)(2,1)} custom-call(bf16[192,1024]{1,0:T(8,128)(2,1)} %bitcast.11), custom_call_target="tpu_custom_call" | custom-call | tf_op jit(solution)/shard_map/spread3/pallas_call | solution.py:297
  59.3 0.0 copy-done.3
  59.3 0.0 copy-done.4
  59.4 0.0 copy-start
  59.4 1.1 copy-done
  60.5 0.0 copy-start.2
  60.5 1.0 copy-done.2
  61.5 0.0 copy-start.5
  61.5 0.0 copy-start.1
  61.5 53.8 %moments.1 = f32[66,192]{1,0:T(8,128)S(1)} custom-call(s32[300]{0:T(512)S(1)} %copy-done.3, s32[6]{0:T(128)S(1)} %copy-done.4, f32[2048,1024]{1,0:T(8,128)} %cos_hbm.1, bf16[192,2048]{1,0:T(8,128)(2,1)S(1)} %copy-done, bf16[192,1024]{1,0:T(8,128)(2,1)S(1)} %bitcast.12), custom_call_target="tpu_custom_call" | custom-call | tf_op jit(solution)/shard_map/moments/pallas_call | solution.py:181
  115.3 0.0 copy-done.5
  115.3 1.1 convolution_bitcast_fusion.x
  116.4 26.9 %sum4.1 = f32[32,8,192]{2,1,0:T(8,128)} custom-call(f32[32,8,192]{2,1,0:T(8,128)} %convolution_bitcast_fusion.x), custom_call_target="tpu_custom_call" | custom-call | tf_op jit(solution)/shard_map/sum4/pallas_call | solution.py:360
  143.3 1.0 slice.3
  144.3 0.7 reshape.19
  145.0 0.0 copy-done.1
  145.0 0.9 copy.11
Async XLA Ops:
  14.8 44.6 %copy-start.3 = (s32[300]{0:T(512)S(1)}, s32[300]{0:T(512)}, u32[]{:S(2)}) copy-start(s32[300]{0:T(512)} %constant.6.clone.table) | copy-start | bytes 3604
  14.8 44.6 %copy-start.4 = (s32[6]{0:T(128)S(1)}, s32[6]{0:T(128)}, u32[]{:S(2)}) copy-start(s32[6]{0:T(128)} %constant.7.clone.counts) | copy-start | bytes 76
  59.4 1.1 copy-start
  60.5 1.0 copy-start.2
  61.5 53.8 %copy-start.5 = (f32[256,66]{1,0:T(8,128)S(1)}, f32[256,66]{1,0:T(8,128)}, u32[]{:S(2)}) copy-start(f32[256,66]{1,0:T(8,128)} %constant.8.clone) | copy-start | bytes 202756
  61.5 83.5 %copy-start.1 = (bf16[192,2048]{1,0:T(8,128)(2,1)S(1)}, bf16[192,2048]{1,0:T(8,128)(2,1)}, u32[]{:S(2)}) copy-start(bf16[192,2048]{1,0:T(8,128)(2,1)} %spread3.1.ft) | copy-start | bytes 2359300

commit v3 on v2

--- a/solution.py
+++ b/solution.py
@@ -23,10 +23,10 @@
     top = LMIN + L - 1
     each = -(-L // devices)
     a = [math.comb(2 * k, k) / 4.0**k for k in range(top + 1)]
-    out = np.zeros((devices * 8, LEVELS))
+    out = np.zeros((devices * each, LEVELS))
     for l in range(LMIN, top + 1):
         owner, place = divmod(l - LMIN, each)
-        row = out[owner * 8 + place]
+        row = out[owner * each + place]
         for k in range(l + 1):
             row[abs(l - 2 * k)] += a[k] * a[l - k]
         row *= (2 * l + 1) / npix
@@ -291,7 +291,7 @@
 
 def spread(block, n_q, collective_id):
     maps, width = block.shape
-    pieces = min(4, width // 128)
+    pieces = width // 128
     vmem = pl.BlockSpec(memory_space=pltpu.VMEM)
     sems = pltpu.SemaphoreType.DMA((pieces,))
     return pl.pallas_call(
@@ -351,6 +351,99 @@
     each(lambda k: gather(k, lax.rem(me - k + n, n)).wait_recv())
     each(lambda k: scatter(k).wait_send())
     each(lambda k: gather(k, me).wait_send())
+
+
+def pair_kernel(
+    n, place_of, device_of, x, out, from_pair, pair_sum, landed, result,
+    send1, recv1, send2, recv2, send3, recv3, send4, recv4,
+):
+    me = place_of()
+    m = n // 2
+    side, spot = me % 2, me // 2
+    partner = device_of(me + 1 - 2 * side)
+
+    def member(k):
+        return device_of(lax.rem(spot + k, m) * 2 + side)
+
+    def copy(src, dst, send, recv, device):
+        return pltpu.make_async_remote_copy(
+            src_ref=src, dst_ref=dst, send_sem=send, recv_sem=recv,
+            device_id=device, device_id_type=MESH,
+        )
+
+    def first(k):
+        j = lax.rem(spot + k, m)
+        return copy(x.at[2 * j + 1 - side], from_pair.at[j], send1.at[k - 1], recv1.at[k - 1], partner)
+
+    def second(k):
+        return copy(pair_sum.at[k - 1], landed.at[k - 1], send2.at[k - 1], recv2.at[k - 1], member(k))
+
+    def third(k, slot):
+        return copy(result, out.at[slot], send3.at[k - 1], recv3.at[k - 1], member(k))
+
+    def fourth(k, parity):
+        slot = lax.rem(spot - k + m, m) * 2 + parity
+        src = result if k == 0 else out.at[slot]
+        return copy(src, out.at[slot], send4.at[k], recv4.at[k], partner)
+
+    barrier = pltpu.get_barrier_semaphore()
+    pl.semaphore_signal(barrier, inc=1, device_id=partner, device_id_type=MESH)
+    for k in range(1, m):
+        pl.semaphore_signal(barrier, inc=1, device_id=member(k), device_id_type=MESH)
+    pl.semaphore_wait(barrier, m)
+    for k in range(1, m + 1):
+        first(k).start()
+    for k in range(1, m):
+        j = lax.rem(spot + k, m)
+        first(k).wait_recv()
+        pair_sum[k - 1] = x[2 * j + side] + from_pair[j]
+        second(k).start()
+    first(m).wait_recv()
+    total = x[me] + from_pair[spot]
+    for k in range(1, m):
+        second(k).wait_recv()
+        total = total + landed[k - 1]
+    result[...] = total.astype(result.dtype)
+    for k in range(1, m):
+        third(k, me).start()
+    fourth(0, side).start()
+    out[me] = result[...]
+    for k in range(1, m):
+        third(k, lax.rem(spot - k + m, m) * 2 + side).wait_recv()
+        fourth(k, side).start()
+    for k in range(m):
+        fourth(k, 1 - side).wait_recv()
+    for k in range(1, m + 1):
+        first(k).wait_send()
+    for k in range(1, m):
+        second(k).wait_send()
+        third(k, me).wait_send()
+    for k in range(m):
+        fourth(k, side).wait_send()
+
+
+def pair_sum_and_share(x, dtype, place_of, device_of, collective_id):
+    n, rows, cols = x.shape
+    m = n // 2
+    vmem = pl.BlockSpec(memory_space=pltpu.VMEM)
+    whole, rest = pltpu.SemaphoreType.DMA((m,)), pltpu.SemaphoreType.DMA((m - 1,))
+    return pl.pallas_call(
+        functools.partial(pair_kernel, n, place_of, device_of),
+        out_shape=jax.ShapeDtypeStruct(x.shape, dtype),
+        in_specs=[vmem],
+        out_specs=vmem,
+        scratch_shapes=[
+            pltpu.VMEM((m, rows, cols), x.dtype),
+            pltpu.VMEM((m - 1, rows, cols), x.dtype),
+            pltpu.VMEM((m - 1, rows, cols), x.dtype),
+            pltpu.VMEM((rows, cols), dtype),
+            whole, whole, rest, rest, rest, rest, whole, whole,
+        ],
+        compiler_params=pltpu.CompilerParams(
+            collective_id=collective_id, has_side_effects=True
+        ),
+        name="sum%d" % collective_id,
+    )(x)
 
 
 def sum_and_share(x, dtype, place_of, device_of, collective_id):
@@ -380,7 +473,7 @@
     n_q = n_cols // 2
     sky_rows = spread(sky_maps.T, n_q, 1)
     partial_value = jnp.dot(sky_rows, inverse_cov, preferred_element_type=jnp.float32)
-    column_maps = sum_and_share(
+    column_maps = pair_sum_and_share(
         partial_value.reshape(n_rows, maps // n_rows, cols_here),
         jnp.bfloat16,
         lambda: lax.axis_index("prow"),
@@ -393,13 +486,13 @@
     matrix, each = transform_matrix(npix, devices)
     partial_spectra = jnp.dot(jnp.asarray(matrix), moments, precision=lax.Precision.HIGHEST)
     shared = sum_and_share(
-        partial_spectra.reshape(devices, 8, maps),
+        partial_spectra.reshape(devices, each, maps),
         jnp.float32,
         lambda: lax.axis_index("prow") * n_cols + lax.axis_index("pcol"),
         lambda i: (i // n_cols, lax.rem(i, n_cols)),
         4,
     )
-    spectra = shared[:, :each].reshape(devices * each, maps)[:L]
+    spectra = shared.reshape(devices * each, maps)[:L]
     return (row_maps.T, spectra)
 
 

time: 146 us -> 134 us (0.918)
  Pallas kernels: 135 us -> 123 us
    pallas_call x2 -> x1, Pallas kernels: 55.1 us -> 16.2 us  [sum_and_share(): pl.pallas_call(functools.partial(sum_kernel, n, place_of, device_of), out...]
    pallas_call x0 -> x1, Pallas kernels: none -> 24.7 us  [pair_sum_and_share(): pl.pallas_call(functools.partial(pair_kernel, n, place_of, device_of), ou...]
    pallas_call x2, Pallas kernels: 26.1 us -> 28.1 us  [spread(): pl.pallas_call(functools.partial(spread_kernel, n_q), out_shape=jax.Shape...]
    reshape x1 -> x2, local copies, waits for them, and re-layouts: 0.68 us -> 2.18 us  [the longest x1 1.51 us: per_device(): spectra = shared.reshape(devices * each, maps)[:L]]
where the time goes in v3:
time: 134 us; the launch traced here: 133 us
  Pallas kernels  123 us (92%)
  local copies, waits for them, and re-layouts  5.21 us (4%)
  matrix products  4.5 us (3%)
    pallas_call x1, Pallas kernels, spectra_moments(): pl.pallas_call(functools.partial(moments_kernel, stride), out_shape=jax.S...  53.8 us
    pallas_call x2, Pallas kernels, spread(): pl.pallas_call(functools.partial(spread_kernel, n_q), out_shape=jax.Shape...  28.1 us
    pallas_call x1, Pallas kernels, pair_sum_and_share(): pl.pallas_call(functools.partial(pair_kernel, n, place_of, device_of), ou...  24.7 us
    pallas_call x1, Pallas kernels, sum_and_share(): pl.pallas_call(functools.partial(sum_kernel, n, place_of, device_of), out...  16.2 us
    dot_general x1, matrix products, per_device(): jnp.dot(sky_rows, inverse_cov, preferred_element_type=jnp.float32)  4.3 us
    unnamed x13, local copies, waits for them, and re-layouts  3.02 us

profile of v3, /device:TPU:0, one launch (start us, length us, event | category | flops | bytes accessed | tf_op | source)
XLA Modules:
  0.0 133.2 jit_solution(6837945594360187986)
XLA Ops:
  0.6 14.8 %spread1.1 = bf16[192,2048]{1,0:T(8,128)(2,1)} custom-call(bf16[192,1024]{1,0:T(8,128)(2,1)} %bitcast.12), custom_call_target="tpu_custom_call" | custom-call | tf_op jit(solution)/shard_map/spread1/pallas_call | solution.py:297
  15.5 0.0 copy-start.3
  15.5 0.0 copy-start.4
  15.5 4.3 %fusion = f32[192,1024]{1,0:T(8,128)} fusion(bf16[192,2048]{1,0:T(8,128)(2,1)} %spread1.1, bf16[2048,1024]{1,0:T(8,128)(2,1)} %param.6), kind=kOutput, calls=%fused_computation | convolution fusion | flops 805306368 | bytes 5767168 | tf_op jit(solution)/shard_map/dot_general | solution.py:475
  19.8 24.7 %sum2.1 = bf16[4,48,1024]{2,1,0:T(8,128)(2,1)} custom-call(f32[4,48,1024]{2,1,0:T(8,128)} %bitcast.11), custom_call_target="tpu_custom_call" | custom-call | tf_op jit(solution)/shard_map/sum2/pallas_call | solution.py:430
  44.5 13.2 %spread3.1.ft = bf16[192,2048]{1,0:T(8,128)(2,1)} custom-call(bf16[192,1024]{1,0:T(8,128)(2,1)} %bitcast.9), custom_call_target="tpu_custom_call" | custom-call | tf_op jit(solution)/shard_map/spread3/pallas_call | solution.py:297
  57.7 0.0 copy-done.3
  57.8 0.0 copy-done.4
  57.8 0.0 copy-start
  57.8 1.1 copy-done
  58.9 0.0 copy-start.2
  58.9 1.0 copy-done.2
  59.9 0.0 copy-start.5
  59.9 0.0 copy-start.1
  59.9 53.8 %moments.1 = f32[66,192]{1,0:T(8,128)S(1)} custom-call(s32[300]{0:T(512)S(1)} %copy-done.3, s32[6]{0:T(128)S(1)} %copy-done.4, f32[2048,1024]{1,0:T(8,128)} %cos_hbm.1, bf16[192,2048]{1,0:T(8,128)(2,1)S(1)} %copy-done, bf16[192,1024]{1,0:T(8,128)(2,1)S(1)} %bitcast.10), custom_call_target="tpu_custom_call" | custom-call | tf_op jit(solution)/shard_map/moments/pallas_call | solution.py:181
  113.7 0.0 copy-done.5
  113.7 0.2 fusion.1
  113.9 0.7 reshape.18.x
  114.6 16.2 %sum4.1 = f32[32,2,192]{2,1,0:T(2,128)} custom-call(f32[32,2,192]{2,1,0:T(2,128)} %reshape.18.x), custom_call_target="tpu_custom_call" | custom-call | tf_op jit(solution)/shard_map/sum4/pallas_call | solution.py:453
  130.8 1.5 %reshape.19 = f32[64,192]{1,0:T(8,128)} reshape(f32[32,2,192]{2,1,0:T(2,128)} %sum4.1) | data formatting | bytes 98304 | tf_op jit(solution)/shard_map/reshape | solution.py:495
  132.3 0.0 copy-done.1
  132.3 0.9 copy.9
Async XLA Ops:
  15.5 42.3 %copy-start.3 = (s32[300]{0:T(512)S(1)}, s32[300]{0:T(512)}, u32[]{:S(2)}) copy-start(s32[300]{0:T(512)} %constant.6.clone.table) | copy-start | bytes 3604
  15.5 42.3 %copy-start.4 = (s32[6]{0:T(128)S(1)}, s32[6]{0:T(128)}, u32[]{:S(2)}) copy-start(s32[6]{0:T(128)} %constant.7.clone.counts) | copy-start | bytes 76
  57.8 1.1 copy-start
  58.9 1.0 copy-start.2
  59.9 53.8 %copy-start.5 = (f32[64,66]{1,0:T(8,128)S(1)}, f32[64,66]{1,0:T(8,128)}, u32[]{:S(2)}) copy-start(f32[64,66]{1,0:T(8,128)} %constant.8.clone) | copy-start | bytes 50692
  59.9 72.4 %copy-start.1 = (bf16[192,2048]{1,0:T(8,128)(2,1)S(1)}, bf16[192,2048]{1,0:T(8,128)(2,1)}, u32[]{:S(2)}) copy-start(bf16[192,2048]{1,0:T(8,128)(2,1)} %spread3.1.ft) | copy-start | bytes 2359300
